TPU v7x, 32 devices: a whole 2x2x4 slice. The times are simulated.
32 devices in a mesh: head: 2 (over y), seq: 16 (over z, x, core).
Axes of the slice: x: 2, y: 2, z: 4, core: 2. Of those that a mesh axis runs over, the one named last changes fastest.
Arguments:
- queries: bfloat16 [2048, 4096], P(('seq', 'head')), may hold values from -20 to 20
- keys: bfloat16 [2048, 1024], P(('seq', 'head')), may hold values from -5 to 5
- values: bfloat16 [2048, 1024], P(('seq', 'head')), may hold values from -6 to 6
Outputs:
- attended: bfloat16 [2048, 4096], P(('seq', 'head'))
All inputs are finite; a program needn't handle non-finite values.
Results may differ from a plain program's by a relative error of at most 0.0041.
Values may be sent and summed in bfloat16 or wider, within the bound.
No kernel may reach another device: no remote copies, remote signals or barrier semaphores. Data moves between devices by JAX's collectives and lax.ppermute only.
A program may use at most 64 MiB of HBM per device.

v0:
```python
import math
import jax
import jax.numpy as jnp
from jax import lax
from jax.sharding import PartitionSpec as P

HEAD_DIM = 128


def update_state(state, query_half, query_pos, key_piece, value_piece, key_pos):
    largest, total, summed = state
    score = jnp.einsum("tkgd,pkd->tkgp", query_half, key_piece, preferred_element_type=jnp.float32)
    score = score / math.sqrt(query_half.shape[-1])
    allowed = (key_pos[None, :] <= query_pos[:, None])[:, None, None, :]
    score = jnp.where(allowed, score, jnp.float32(-1e30))
    new_largest = jnp.maximum(largest, jnp.max(score, axis=-1))
    weight = jnp.where(allowed, jnp.exp(score - new_largest[..., None]), jnp.float32(0.0))
    total = jnp.sum(weight, axis=-1)
    product = jnp.einsum(
        "tkgp,pkd->tkgd",
        weight.astype(jnp.bfloat16),
        value_piece,
        preferred_element_type=jnp.float32,
    )
    summed = product
    return (new_largest, total, summed)


def on_device(queries, keys, values):
    q_local, k_local, v_local = (
        lax.all_to_all(queries, "head", split_axis=1, concat_axis=0, tiled=True),
        lax.all_to_all(keys, "head", split_axis=1, concat_axis=0, tiled=True),
        lax.all_to_all(values, "head", split_axis=1, concat_axis=0, tiled=True),
    )
    tokens = q_local.shape[0]
    half = tokens // 2
    kv_local = k_local.shape[1] // HEAD_DIM
    group = q_local.shape[1] // k_local.shape[1]
    index = lax.axis_index("seq")
    offsets = jnp.arange(half, dtype=jnp.int32)
    later = q_local[half:]
    early_pos = index * tokens + offsets
    later_pos = index * tokens + half + offsets
    query_pos = jnp.stack([early_pos, later_pos])
    halves = jnp.stack([q_local[:half], later]).reshape(2, half, kv_local, group, HEAD_DIM)
    start_state = (
        jnp.full((2, half, kv_local, group), -1e30, jnp.float32),
        jnp.zeros((2, half, kv_local, group), jnp.float32),
        jnp.zeros((2, half, kv_local, group, HEAD_DIM), jnp.float32),
    )
    start = jnp.int32(0)
    key_piece = lax.all_gather(k_local, "seq", axis=0, tiled=True)
    value_piece = lax.all_gather(v_local, "seq", axis=0, tiled=True)
    rows = key_piece.shape[0]
    key_piece = key_piece.reshape(rows, kv_local, HEAD_DIM)
    value_piece = value_piece.reshape(rows, kv_local, HEAD_DIM)
    key_pos = jnp.arange(rows, dtype=jnp.int32)
    results = []
    for which in range(2):
        state = (start_state[0][which], start_state[1][which], start_state[2][which])
        needed = start <= query_pos[which, half - 1]

        def run(current, which=which):
            return update_state(
                current, halves[which], query_pos[which], key_piece, value_piece, key_pos
            )

        def keep(current):
            return current

        results.append(lax.cond(needed, run, keep, state))
    total = jnp.stack([results[0][1], results[1][1]])
    summed = jnp.stack([results[0][2], results[1][2]])
    result = (summed / total[..., None]).reshape(2, half, q_local.shape[1]).astype(jnp.bfloat16)
    later_out = result[1]
    combined = jnp.concatenate([result[0], later_out], axis=0)
    return lax.all_to_all(combined, "head", split_axis=0, concat_axis=1, tiled=True)


def solution(mesh):
    return jax.shard_map(
        on_device,
        mesh=mesh,
        in_specs=(P(("seq", "head"), None), P(("seq", "head"), None), P(("seq", "head"), None)),
        out_specs=P(("seq", "head"), None),
        check_vma=False,
    )
```

profile of v0, /device:TPU:0, one launch (start us, length us, event | category | flops | bytes accessed | tf_op | source)
XLA Modules:
  0.0 142.9 jit_solution(106555980706747682)
XLA Ops:
  6.5 0.9 copy.81
  7.5 8.6 %all_to_all.73 = bf16[64,2,512]{2,0,1:T(8,128)(2,1)} all-to-all(bf16[64,2,512]{2,0,1:T(8,128)(2,1)S(1)} %bitcast.111), channel_id=1, replica_groups=mesh['head'=2,'seq'=16] {'head'}, dimensions={1} | all-to-all | bytes 262144 | tf_op jit(solution)/shard_map/all_to_all | solution.py:32
  16.2 0.9 copy.80
  17.1 7.5 %all_to_all.74 = bf16[64,2,512]{2,0,1:T(8,128)(2,1)} all-to-all(bf16[64,2,512]{2,0,1:T(8,128)(2,1)S(1)} %bitcast.112), channel_id=1, replica_groups=mesh['head'=2,'seq'=16] {'head'}, dimensions={1} | all-to-all | bytes 262144 | tf_op jit(solution)/shard_map/all_to_all | solution.py:33
  24.6 1.9 %copy.79 = bf16[8,2,8,2048]{3,2,0,1:T(8,128)(2,1)} copy(bf16[8,2,8,2048]{3,2,1,0:T(8,128)(2,1)} %bitcast.108) | data formatting | bytes 1048576 | tf_op jit(solution)/shard_map/all_to_all | solution.py:31
  26.5 3.5 %all-to-all-start = ((bf16[64,2,2048]{2,0,1:T(8,128)(2,1)}), bf16[64,2,2048]{2,0,1:T(8,128)(2,1)S(1)}, u32[]{:S(2)}, u32[]{:S(2)}) async-start(bf16[64,2,2048]{2,0,1:T(8,128)(2,1)} %bitcast.98), calls=%async_computation | async-start | bytes 1048576 | tf_op jit(solution)/shard_map/all_to_all | solution.py:31
  30.0 0.6 slice.29
  31.4 0.6 slice.26
  32.6 4.0 %all-to-all-done = bf16[64,2,2048]{2,0,1:T(8,128)(2,1)S(1)} async-done(((bf16[64,2,2048]{2,0,1:T(8,128)(2,1)}), bf16[64,2,2048]{2,0,1:T(8,128)(2,1)S(1)}, u32[]{:S(2)}, u32[]{:S(2)}) %all-to-all-start) | async-done | bytes 524320 | tf_op jit(solution)/shard_map/all_to_all | solution.py:31
  36.6 0.2 stack.42
  37.2 21.2 %all-gather.3.cloned.1.call-done = bf16[2048,512]{1,0:T(8,128)(2,1)} async-done(((bf16[128,512]{1,0:T(8,128)(2,1)}), bf16[2048,512]{1,0:T(8,128)(2,1)}) %all-gather.3.cloned.1.call-update) | async-done | bytes 2097168 | tf_op jit(solution)/shard_map/all_gather | solution.py:52
  58.4 2.9 %copy.49 = bf16[2048,512]{0,1:T(8,128)(2,1)S(1)} copy(bf16[2048,512]{1,0:T(8,128)(2,1)} %all-gather.3.cloned.1.call-done) | data formatting | bytes 4194304 | tf_op jit(solution)/shard_map/all_gather | solution.py:52
  61.3 39.4 %all-gather.5.cloned.1.call-done = bf16[2048,512]{1,0:T(8,128)(2,1)} async-done(((bf16[128,512]{1,0:T(8,128)(2,1)}), bf16[2048,512]{1,0:T(8,128)(2,1)}) %all-gather.5.cloned.1.call-update) | async-done | bytes 2097168 | tf_op jit(solution)/shard_map/all_gather | solution.py:53
  100.7 4.0 %copy.51 = bf16[2048,512]{0,1:T(8,128)(2,1)} copy(bf16[2048,512]{1,0:T(8,128)(2,1)} %all-gather.5.cloned.1.call-done) | data formatting | bytes 4194304 | tf_op jit(solution)/shard_map/all_gather | solution.py:53
  104.7 8.9 %conditional.2 = (f32[1,64,4,4]{1,3,2,0:T(4,128)S(1)}, f32[1,64,2048]{2,1,0:T(8,128)S(1)}) conditional(s32[]{:T(128)} %bitcast.12, () %tuple.29, (s32[2048]{0:T(1024)S(1)}, s32[]{:T(128)}, s32[64]{0:T(128)S(1)}, bf16[2,64,4,4,128]{4,3,2,1,0:T(4,128)(2,1)S(1)}, bf16[2048,4,128]{0,2,1:T(8,128)(2,1)S(1)}, ...), branch_computations={%region_0.0_spmd, %region_1.4_spmd} | conditional | flops 1101134848 | bytes 42238768 | solution.py:71
  105.1 1.7 %fusion = (f32[64,4,4]{0,2,1:T(4,128)S(1)}, f32[4,2048,64,4]{1,2,3,0:T(8,128)S(1)}) fusion(pred[64,2048]{1,0:T(8,128)(4,1)S(1)} %broadcast_compare_fusion, bf16[2,64,4,4,128]{4,1,3,2,0:T(8,128)(2,1)S(1)} %copy.52, bf16[2048,4,128]{0,2,1:T(8,128)(2,1)S(1)} %get-tuple-element.97), kind=kOutput, calls=%fused_computation.2 | convolution fusion | flops 543161344 | bytes 10883072 | tf_op jit(solution)/shard_map/cond/branch_1_fun/tkgd,pkd->tkgp/dot_general | solution.py:12
  106.8 1.9 %fusion.9 = f32[64,4,4,128]{3,0,2,1:T(8,128)S(1)} fusion(bf16[2048,4,128]{0,2,1:T(8,128)(2,1)S(1)} %copy-done, f32[4,2048,64,4]{1,2,3,0:T(8,128)S(1)} %get-tuple-element.106, f32[64,4,4]{0,2,1:T(4,128)S(1)} %broadcast_maximum_fusion, pred[64,2048]{1,0:T(8,128)(4,1)S(1)} %broadcast_compare_fusion), kind=kOutput, calls=%fused_computation.10 | convolution fusion | flops 547356672 | bytes 11145216 | tf_op jit(solution)/shard_map/cond/branch_1_fun/tkgp,pkd->tkgd/dot_general | solution.py:19
  108.7 2.5 %fusion.2 = f32[64,4,4]{0,2,1:T(4,128)S(1)} fusion(f32[4,2048,64,4]{1,2,3,0:T(8,128)S(1)} %get-tuple-element.106, f32[64,4,4]{0,2,1:T(4,128)S(1)} %broadcast_maximum_fusion, pred[64,2048]{1,0:T(8,128)(4,1)S(1)} %broadcast_compare_fusion), kind=kLoop, calls=%fused_computation.4 | loop fusion | flops 10484736 | bytes 8527872 | tf_op jit(solution)/shard_map/cond/branch_1_fun/reduce_sum | solution.py:18
  111.2 1.1 copy.45
  112.4 1.3 stack.31
  113.6 8.0 %conditional.3 = (f32[1,64,4,4]{1,3,2,0:T(4,128)S(1)}, f32[1,64,2048]{2,1,0:T(8,128)}) conditional(s32[]{:T(128)} %bitcast.20, () %tuple.31, (s32[2048]{0:T(1024)S(1)}, s32[]{:T(128)}, s32[64]{0:T(128)S(1)}, bf16[2,64,4,4,128]{4,3,2,1,0:T(4,128)(2,1)S(1)}, bf16[2048,4,128]{0,2,1:T(8,128)(2,1)S(1)}, /*index=5*/bf16[2048,4,128]{0,2,1:T(8,128)(2,1)}) %tuple.56), branch_computations={%region_4.5_spmd, %region_5.8_spmd} | conditional | flops 1101134848 | bytes 42238768 | solution.py:71
  114.1 1.7 %fusion.17 = (f32[64,4,4]{0,2,1:T(4,128)S(1)}, f32[4,2048,64,4]{1,2,3,0:T(8,128)S(1)}) fusion(pred[64,2048]{1,0:T(8,128)(4,1)S(1)} %broadcast_compare_fusion.1, bf16[2,64,4,4,128]{4,1,3,2,0:T(8,128)(2,1)S(1)} %copy.55, bf16[2048,4,128]{0,2,1:T(8,128)(2,1)S(1)} %get-tuple-element.103), kind=kOutput, calls=%fused_computation.20 | convolution fusion | flops 543161344 | bytes 10883072 | tf_op jit(solution)/shard_map/cond/branch_1_fun/tkgd,pkd->tkgp/dot_general | solution.py:12
  115.8 1.9 %fusion.26 = f32[64,4,4,128]{3,0,2,1:T(8,128)S(1)} fusion(bf16[2048,4,128]{0,2,1:T(8,128)(2,1)S(1)} %copy-done.1, f32[4,2048,64,4]{1,2,3,0:T(8,128)S(1)} %get-tuple-element.108, f32[64,4,4]{0,2,1:T(4,128)S(1)} %broadcast_maximum_fusion.1, pred[64,2048]{1,0:T(8,128)(4,1)S(1)} %broadcast_compare_fusion.1), kind=kOutput, calls=%fused_computation.28 | convolution fusion | flops 547356672 | bytes 11145216 | tf_op jit(solution)/shard_map/cond/branch_1_fun/tkgp,pkd->tkgd/dot_general | solution.py:19
  117.8 2.5 %fusion.19 = f32[64,4,4]{0,2,1:T(4,128)S(1)} fusion(f32[4,2048,64,4]{1,2,3,0:T(8,128)S(1)} %get-tuple-element.108, f32[64,4,4]{0,2,1:T(4,128)S(1)} %broadcast_maximum_fusion.1, pred[64,2048]{1,0:T(8,128)(4,1)S(1)} %broadcast_compare_fusion.1), kind=kLoop, calls=%fused_computation.22 | loop fusion | flops 10484736 | bytes 8527872 | tf_op jit(solution)/shard_map/cond/branch_1_fun/reduce_sum | solution.py:18
  120.3 0.3 copy.46
  120.7 1.0 stack.35
  121.7 0.2 copy.58
  121.9 0.6 div.21
  122.5 0.4 div.22
  122.9 1.2 fusion.34
  124.2 11.1 %all_to_all.75 = bf16[2,64,2048]{2,1,0:T(8,128)(2,1)S(1)} all-to-all(bf16[2,64,2048]{2,1,0:T(8,128)(2,1)S(1)} %bitcast.106), channel_id=1, replica_groups=mesh['head'=2,'seq'=16] {'head'}, dimensions={0} | all-to-all | bytes 1048576 | tf_op jit(solution)/shard_map/all_to_all | solution.py:77
  135.2 0.8 copy.75
  (29 shorter events, 1.2 us)
Async XLA Ops:
  6.5 51.8 %all-gather.3.cloned.1.call-start = ((), (), s32[]{:S(2)}) async-start(), calls=%async_computation.4 | async-start | bytes 2228224 | tf_op jit(solution)/shard_map/all_gather | solution.py:52
  16.1 84.6 %all-gather.5.cloned.1.call-start = ((), (), s32[]{:S(2)}) async-start(), calls=%async_computation.5 | async-start | bytes 2228224 | tf_op jit(solution)/shard_map/all_gather | solution.py:53
  26.5 10.1 %all-to-all-start = ((bf16[64,2,2048]{2,0,1:T(8,128)(2,1)}), bf16[64,2,2048]{2,0,1:T(8,128)(2,1)S(1)}, u32[]{:S(2)}, u32[]{:S(2)}) async-start(bf16[64,2,2048]{2,0,1:T(8,128)(2,1)} %bitcast.98), calls=%async_computation | async-start | bytes 1048576 | tf_op jit(solution)/shard_map/all_to_all | solution.py:31
  105.0 1.7 %copy-start = (bf16[2048,4,128]{0,2,1:T(8,128)(2,1)S(1)}, bf16[2048,4,128]{0,2,1:T(8,128)(2,1)}, u32[]{:S(2)}) copy-start(bf16[2048,4,128]{0,2,1:T(8,128)(2,1)} %get-tuple-element.98) | copy-start | bytes 6291460 | tf_op jit(solution)/shard_map/cond
  114.1 1.7 %copy-start.1 = (bf16[2048,4,128]{0,2,1:T(8,128)(2,1)S(1)}, bf16[2048,4,128]{0,2,1:T(8,128)(2,1)}, u32[]{:S(2)}) copy-start(bf16[2048,4,128]{0,2,1:T(8,128)(2,1)} %get-tuple-element.104) | copy-start | bytes 6291460 | tf_op jit(solution)/shard_map/cond
Sparse Core Ops, SparseCore 0:
  16.2 42.0 all-gather.2
  60.5 40.1 all-gather.4
where the time goes:
time: 144 us; the launch traced here: 143 us
  waiting for transfers between devices  64.6 us (45%)
  blocking collectives  27.2 us (19%)
  local copies, waits for them, and re-layouts  18.5 us (13%)
  between operations  14.8 us (10%)
  matrix products  7.21 us (5%)
  other arithmetic  6.63 us (5%)
  starting transfers between devices  3.53 us (2%)
    all_gather x1, waiting for transfers between devices, on_device(): value_piece = lax.all_gather(v_local, 'seq', axis=0, tiled=True)  39.4 us
    all_gather x1, waiting for transfers between devices, on_device(): key_piece = lax.all_gather(k_local, 'seq', axis=0, tiled=True)  21.2 us
    all_to_all x1, blocking collectives, on_device(): lax.all_to_all(combined, 'head', split_axis=0, concat_axis=1, tiled=True)  11.1 us
    all_to_all x1, blocking collectives, on_device(): lax.all_to_all(keys, 'head', split_axis=1, concat_axis=0, tiled=True)  8.64 us
    all_to_all x1, blocking collectives, on_device(): lax.all_to_all(values, 'head', split_axis=1, concat_axis=0, tiled=True)  7.52 us
    reduce_sum x2, other arithmetic, update_state(): total = jnp.sum(weight, axis=-1)  5.08 us
    all_to_all x1, waiting for transfers between devices, on_device(): lax.all_to_all(queries, 'head', split_axis=1, concat_axis=0, tiled=True)  3.99 us
    all_gather x1, local copies, waits for them, and re-layouts, on_device(): value_piece = lax.all_gather(v_local, 'seq', axis=0, tiled=True)  3.95 us
  transfers between devices with their start and end apart: 3, of which 3 were waited for; matrix products, arithmetic and copies ran while one was open for 5% of the time, Pallas kernels for 0%

commit v1 on v0

--- a/solution.py
+++ b/solution.py
@@ -49,8 +49,11 @@
         jnp.zeros((2, half, kv_local, group, HEAD_DIM), jnp.float32),
     )
     start = jnp.int32(0)
-    key_piece = lax.all_gather(k_local, "seq", axis=0, tiled=True)
-    value_piece = lax.all_gather(v_local, "seq", axis=0, tiled=True)
+    key_piece, value_piece = jnp.split(
+        lax.all_gather(jnp.concatenate([k_local, v_local], axis=1), "seq", axis=0, tiled=True),
+        [k_local.shape[1]],
+        axis=1,
+    )
     rows = key_piece.shape[0]
     key_piece = key_piece.reshape(rows, kv_local, HEAD_DIM)
     value_piece = value_piece.reshape(rows, kv_local, HEAD_DIM)

time: 144 us -> 124 us (0.86)
  waiting for transfers between devices: 64.6 us -> 46.2 us
  blocking collectives: 27.2 us -> 17.9 us
  starting transfers between devices: 3.53 us -> 7.75 us
  local copies, waits for them, and re-layouts: 18.5 us -> 21.5 us
    all_gather x2 -> x1, waiting for transfers between devices: 60.6 us -> 38.7 us  [on_device(): lax.all_gather(jnp.concatenate([k_local, v_local], axis=1), 'seq', axis=0...]
    split x0 -> x3, local copies, waits for them, and re-layouts: none -> 9.17 us  [on_device(): jnp.split(lax.all_gather(jnp.concatenate([k_local, v_local], axis=1), 'se...]
    all_to_all x1 -> x0, blocking collectives: 8.64 us -> none  [on_device(): lax.all_to_all(keys, 'head', split_axis=1, concat_axis=0, tiled=True)]
    all_gather x2 -> x0, local copies, waits for them, and re-layouts: 6.88 us -> none  [the longest x1 3.95 us: on_device(): value_piece = lax.all_gather(v_local, 'seq', axis=0, tiled=True)]
    all_to_all x0 -> x1, starting transfers between devices: none -> 4.26 us  [on_device(): lax.all_to_all(keys, 'head', split_axis=1, concat_axis=0, tiled=True)]
    all_to_all x0 -> x1, waiting for transfers between devices: none -> 3.64 us  [on_device(): lax.all_to_all(keys, 'head', split_axis=1, concat_axis=0, tiled=True)]
  transfers between devices with their start and end apart: 3 -> 3, of which waited for: 3 -> 3; matrix products, arithmetic and copies ran while one was open for 5% -> 4% of each run, Pallas kernels for 0% -> 0%
where the time goes in v1:
time: 124 us; the launch traced here: 123 us
  waiting for transfers between devices  46.2 us (37%)
  local copies, waits for them, and re-layouts  21.5 us (17%)
  blocking collectives  17.9 us (14%)
  between operations  14.9 us (12%)
  starting transfers between devices  7.75 us (6%)
  other arithmetic  7.36 us (6%)
  matrix products  7.2 us (6%)
    all_gather x1, waiting for transfers between devices, on_device(): lax.all_gather(jnp.concatenate([k_local, v_local], axis=1), 'seq', axis=0...  38.7 us
    all_to_all x1, blocking collectives, on_device(): lax.all_to_all(combined, 'head', split_axis=0, concat_axis=1, tiled=True)  11.1 us
    split x3, local copies, waits for them, and re-layouts, on_device(): jnp.split(lax.all_gather(jnp.concatenate([k_local, v_local], axis=1), 'se...  9.17 us
    all_to_all x1, blocking collectives, on_device(): lax.all_to_all(values, 'head', split_axis=1, concat_axis=0, tiled=True)  6.84 us
    reduce_sum x2, other arithmetic, update_state(): total = jnp.sum(weight, axis=-1)  5.08 us
    all_to_all x1, starting transfers between devices, on_device(): lax.all_to_all(keys, 'head', split_axis=1, concat_axis=0, tiled=True)  4.26 us
    dot_general x2, matrix products, update_state(): jnp.einsum('tkgp,pkd->tkgd', weight.astype(jnp.bfloat16), value_piece, pr...  3.86 us
    all_to_all x1, waiting for transfers between devices, on_device(): lax.all_to_all(queries, 'head', split_axis=1, concat_axis=0, tiled=True)  3.8 us
  transfers between devices with their start and end apart: 3, of which 3 were waited for; matrix products, arithmetic and copies ran while one was open for 4% of the time, Pallas kernels for 0%

profile of v1, /device:TPU:0, one launch (start us, length us, event | category | flops | bytes accessed | tf_op | source)
XLA Modules:
  0.0 123.3 jit_solution(15416918690146007499)
XLA Ops:
  6.5 1.6 %copy.81 = bf16[8,2,8,512]{3,2,0,1:T(8,128)(2,1)} copy(bf16[8,2,8,512]{3,2,1,0:T(8,128)(2,1)} %bitcast.112) | data formatting | bytes 262144 | tf_op jit(solution)/shard_map/all_to_all | solution.py:32
  8.1 4.3 %all-to-all-start.1 = ((bf16[64,2,512]{2,0,1:T(8,128)(2,1)}), bf16[64,2,512]{2,0,1:T(8,128)(2,1)S(1)}, u32[]{:S(2)}, u32[]{:S(2)}) async-start(bf16[64,2,512]{2,0,1:T(8,128)(2,1)} %bitcast.100), calls=%async_computation.1 | async-start | bytes 262144 | tf_op jit(solution)/shard_map/all_to_all | solution.py:32
  12.4 0.9 copy.80
  13.3 3.6 %all-to-all-done.1 = bf16[64,2,512]{2,0,1:T(8,128)(2,1)S(1)} async-done(((bf16[64,2,512]{2,0,1:T(8,128)(2,1)}), bf16[64,2,512]{2,0,1:T(8,128)(2,1)S(1)}, u32[]{:S(2)}, u32[]{:S(2)}) %all-to-all-start.1) | async-done | bytes 131104 | tf_op jit(solution)/shard_map/all_to_all | solution.py:32
  16.9 6.8 %all_to_all.73 = bf16[64,2,512]{2,0,1:T(8,128)(2,1)S(1)} all-to-all(bf16[64,2,512]{2,0,1:T(8,128)(2,1)S(1)} %bitcast.109), channel_id=1, replica_groups=mesh['head'=2,'seq'=16] {'head'}, dimensions={1} | all-to-all | bytes 262144 | tf_op jit(solution)/shard_map/all_to_all | solution.py:33
  23.8 0.7 pad_maximum_fusion.1
  24.5 1.9 %copy.79 = bf16[8,2,8,2048]{3,2,0,1:T(8,128)(2,1)} copy(bf16[8,2,8,2048]{3,2,1,0:T(8,128)(2,1)} %bitcast.108) | data formatting | bytes 1048576 | tf_op jit(solution)/shard_map/all_to_all | solution.py:31
  26.4 3.5 %all-to-all-start = ((bf16[64,2,2048]{2,0,1:T(8,128)(2,1)}), bf16[64,2,2048]{2,0,1:T(8,128)(2,1)S(1)}, u32[]{:S(2)}, u32[]{:S(2)}) async-start(bf16[64,2,2048]{2,0,1:T(8,128)(2,1)} %bitcast.98), calls=%async_computation | async-start | bytes 1048576 | tf_op jit(solution)/shard_map/all_to_all | solution.py:31
  29.9 0.7 slice.29
  31.3 0.7 slice.26
  32.7 3.8 %all-to-all-done = bf16[64,2,2048]{2,0,1:T(8,128)(2,1)S(1)} async-done(((bf16[64,2,2048]{2,0,1:T(8,128)(2,1)}), bf16[64,2,2048]{2,0,1:T(8,128)(2,1)S(1)}, u32[]{:S(2)}, u32[]{:S(2)}) %all-to-all-start) | async-done | bytes 524320 | tf_op jit(solution)/shard_map/all_to_all | solution.py:31
  37.1 38.7 %all-gather.2.cloned.1.call-done = bf16[2048,1024]{1,0:T(8,128)(2,1)} async-done(((bf16[128,1024]{1,0:T(8,128)(2,1)}), bf16[2048,1024]{1,0:T(8,128)(2,1)}) %all-gather.2.cloned.1.call-update) | async-done | bytes 4194320 | tf_op jit(solution)/shard_map/all_gather | solution.py:53
  75.8 3.8 %fusion.35 = (bf16[2048,512]{1,0:T(8,128)(2,1)S(1)}, bf16[2048,512]{1,0:T(8,128)(2,1)}) fusion(bf16[2048,1024]{1,0:T(8,128)(2,1)} %all-gather.2.cloned.1.call-done), kind=kLoop, calls=%fused_computation.50 | loop fusion | bytes 8388608 | tf_op jit(solution)/shard_map/split | solution.py:52
  79.6 2.4 %copy.51 = bf16[2048,512]{0,1:T(8,128)(2,1)} copy(bf16[2048,512]{1,0:T(8,128)(2,1)S(1)} %get-tuple-element.109) | data formatting | bytes 4194304 | tf_op jit(solution)/shard_map/split | solution.py:52
  82.1 2.9 %copy.50 = bf16[2048,512]{0,1:T(8,128)(2,1)S(1)} copy(bf16[2048,512]{1,0:T(8,128)(2,1)} %get-tuple-element.110) | data formatting | bytes 4194304 | tf_op jit(solution)/shard_map/split | solution.py:52
  85.1 8.9 %conditional.2 = (f32[1,64,4,4]{1,3,2,0:T(4,128)S(1)}, f32[1,64,2048]{2,1,0:T(8,128)S(1)}) conditional(s32[]{:T(128)} %bitcast.12, () %tuple.29, (s32[2048]{0:T(1024)S(1)}, s32[]{:T(128)}, s32[64]{0:T(128)S(1)}, bf16[2,64,4,4,128]{4,3,2,1,0:T(4,128)(2,1)S(1)}, bf16[2048,4,128]{0,2,1:T(8,128)(2,1)S(1)}, ...), branch_computations={%region_0.0_spmd, %region_1.4_spmd} | conditional | flops 1101134848 | bytes 42238768 | solution.py:74
  85.4 1.7 %fusion = (f32[64,4,4]{0,2,1:T(4,128)S(1)}, f32[4,2048,64,4]{1,2,3,0:T(8,128)S(1)}) fusion(pred[64,2048]{1,0:T(8,128)(4,1)S(1)} %broadcast_compare_fusion, bf16[2,64,4,4,128]{4,1,3,2,0:T(8,128)(2,1)S(1)} %copy.52, bf16[2048,4,128]{0,2,1:T(8,128)(2,1)S(1)} %get-tuple-element.97), kind=kOutput, calls=%fused_computation.2 | convolution fusion | flops 543161344 | bytes 10883072 | tf_op jit(solution)/shard_map/cond/branch_1_fun/tkgd,pkd->tkgp/dot_general | solution.py:12
  87.1 1.9 %fusion.9 = f32[64,4,4,128]{3,0,2,1:T(8,128)S(1)} fusion(bf16[2048,4,128]{0,2,1:T(8,128)(2,1)S(1)} %copy-done, f32[4,2048,64,4]{1,2,3,0:T(8,128)S(1)} %get-tuple-element.106, f32[64,4,4]{0,2,1:T(4,128)S(1)} %broadcast_maximum_fusion, pred[64,2048]{1,0:T(8,128)(4,1)S(1)} %broadcast_compare_fusion), kind=kOutput, calls=%fused_computation.10 | convolution fusion | flops 547356672 | bytes 11145216 | tf_op jit(solution)/shard_map/cond/branch_1_fun/tkgp,pkd->tkgd/dot_general | solution.py:19
  89.0 2.5 %fusion.2 = f32[64,4,4]{0,2,1:T(4,128)S(1)} fusion(f32[4,2048,64,4]{1,2,3,0:T(8,128)S(1)} %get-tuple-element.106, f32[64,4,4]{0,2,1:T(4,128)S(1)} %broadcast_maximum_fusion, pred[64,2048]{1,0:T(8,128)(4,1)S(1)} %broadcast_compare_fusion), kind=kLoop, calls=%fused_computation.4 | loop fusion | flops 10484736 | bytes 8527872 | tf_op jit(solution)/shard_map/cond/branch_1_fun/reduce_sum | solution.py:18
  91.6 1.1 copy.45
  92.7 1.3 %stack.31 = f32[1,64,2048]{2,1,0:T(8,128)S(1)} reshape(f32[64,4,4,128]{3,2,1,0:T(4,128)} %copy.45) | data formatting | bytes 1048576 | tf_op jit(solution)/shard_map/stack | solution.py:76
  94.0 8.0 %conditional.3 = (f32[1,64,4,4]{1,3,2,0:T(4,128)S(1)}, f32[1,64,2048]{2,1,0:T(8,128)}) conditional(s32[]{:T(128)} %bitcast.20, () %tuple.31, (s32[2048]{0:T(1024)S(1)}, s32[]{:T(128)}, s32[64]{0:T(128)S(1)}, bf16[2,64,4,4,128]{4,3,2,1,0:T(4,128)(2,1)S(1)}, bf16[2048,4,128]{0,2,1:T(8,128)(2,1)S(1)}, /*index=5*/bf16[2048,4,128]{0,2,1:T(8,128)(2,1)}) %tuple.55), branch_computations={%region_4.5_spmd, %region_5.8_spmd} | conditional | flops 1101134848 | bytes 42238768 | solution.py:74
  94.5 1.7 %fusion.17 = (f32[64,4,4]{0,2,1:T(4,128)S(1)}, f32[4,2048,64,4]{1,2,3,0:T(8,128)S(1)}) fusion(pred[64,2048]{1,0:T(8,128)(4,1)S(1)} %broadcast_compare_fusion.1, bf16[2,64,4,4,128]{4,1,3,2,0:T(8,128)(2,1)S(1)} %copy.55, bf16[2048,4,128]{0,2,1:T(8,128)(2,1)S(1)} %get-tuple-element.103), kind=kOutput, calls=%fused_computation.20 | convolution fusion | flops 543161344 | bytes 10883072 | tf_op jit(solution)/shard_map/cond/branch_1_fun/tkgd,pkd->tkgp/dot_general | solution.py:12
  96.2 1.9 %fusion.26 = f32[64,4,4,128]{3,0,2,1:T(8,128)S(1)} fusion(bf16[2048,4,128]{0,2,1:T(8,128)(2,1)S(1)} %copy-done.1, f32[4,2048,64,4]{1,2,3,0:T(8,128)S(1)} %get-tuple-element.108, f32[64,4,4]{0,2,1:T(4,128)S(1)} %broadcast_maximum_fusion.1, pred[64,2048]{1,0:T(8,128)(4,1)S(1)} %broadcast_compare_fusion.1), kind=kOutput, calls=%fused_computation.28 | convolution fusion | flops 547356672 | bytes 11145216 | tf_op jit(solution)/shard_map/cond/branch_1_fun/tkgp,pkd->tkgd/dot_general | solution.py:19
  98.1 2.5 %fusion.19 = f32[64,4,4]{0,2,1:T(4,128)S(1)} fusion(f32[4,2048,64,4]{1,2,3,0:T(8,128)S(1)} %get-tuple-element.108, f32[64,4,4]{0,2,1:T(4,128)S(1)} %broadcast_maximum_fusion.1, pred[64,2048]{1,0:T(8,128)(4,1)S(1)} %broadcast_compare_fusion.1), kind=kLoop, calls=%fused_computation.22 | loop fusion | flops 10484736 | bytes 8527872 | tf_op jit(solution)/shard_map/cond/branch_1_fun/reduce_sum | solution.py:18
  100.6 0.3 copy.46
  101.0 1.0 stack.35
  102.2 0.6 div.21
  102.8 0.4 div.22
  103.2 1.2 fusion.34
  104.5 11.1 %all_to_all.74 = bf16[2,64,2048]{2,1,0:T(8,128)(2,1)S(1)} all-to-all(bf16[2,64,2048]{2,1,0:T(8,128)(2,1)S(1)} %bitcast.106), channel_id=1, replica_groups=mesh['head'=2,'seq'=16] {'head'}, dimensions={0} | all-to-all | bytes 1048576 | tf_op jit(solution)/shard_map/all_to_all | solution.py:80
  115.6 0.8 copy.75
  (29 shorter events, 1.5 us)
Async XLA Ops:
  8.1 8.8 %all-to-all-start.1 = ((bf16[64,2,512]{2,0,1:T(8,128)(2,1)}), bf16[64,2,512]{2,0,1:T(8,128)(2,1)S(1)}, u32[]{:S(2)}, u32[]{:S(2)}) async-start(bf16[64,2,512]{2,0,1:T(8,128)(2,1)} %bitcast.100), calls=%async_computation.1 | async-start | bytes 262144 | tf_op jit(solution)/shard_map/all_to_all | solution.py:32
  12.4 63.5 %all-gather.2.cloned.1.call-start = ((), (), s32[]{:S(2)}) async-start(), calls=%async_computation.4 | async-start | bytes 4456448 | tf_op jit(solution)/shard_map/all_gather | solution.py:53
  26.4 10.1 %all-to-all-start = ((bf16[64,2,2048]{2,0,1:T(8,128)(2,1)}), bf16[64,2,2048]{2,0,1:T(8,128)(2,1)S(1)}, u32[]{:S(2)}, u32[]{:S(2)}) async-start(bf16[64,2,2048]{2,0,1:T(8,128)(2,1)} %bitcast.98), calls=%async_computation | async-start | bytes 1048576 | tf_op jit(solution)/shard_map/all_to_all | solution.py:31
  85.4 1.7 %copy-start = (bf16[2048,4,128]{0,2,1:T(8,128)(2,1)S(1)}, bf16[2048,4,128]{0,2,1:T(8,128)(2,1)}, u32[]{:S(2)}) copy-start(bf16[2048,4,128]{0,2,1:T(8,128)(2,1)} %get-tuple-element.98) | copy-start | bytes 6291460 | tf_op jit(solution)/shard_map/cond
  94.5 1.7 %copy-start.1 = (bf16[2048,4,128]{0,2,1:T(8,128)(2,1)S(1)}, bf16[2048,4,128]{0,2,1:T(8,128)(2,1)}, u32[]{:S(2)}) copy-start(bf16[2048,4,128]{0,2,1:T(8,128)(2,1)} %get-tuple-element.104) | copy-start | bytes 6291460 | tf_op jit(solution)/shard_map/cond
Sparse Core Ops, SparseCore 0:
  24.6 51.1 all-gather.1
